TPU v7x, 32 devices: a whole 2x2x4 slice. The times are simulated.
32 devices in a mesh: win: 4 (over z), step: 8 (over y, x, core).
Axes of the slice: x: 2, y: 2, z: 4, core: 2. Of those that a mesh axis runs over, the one named last changes fastest.
Arguments:
- initial_state: float32 [32, 32, 128], replicated, may hold values from -6 to 6
- source: float32 [4, 8, 32, 32, 128], P('win', 'step'), may hold values from -6 to 6
- absorption: float32 [32, 32, 128], replicated, may hold values from 0.01 to 0.2
Outputs:
- state: float32 [4, 8, 32, 32, 128], P('win', 'step')
All inputs are finite; a program needn't handle non-finite values.
Results may differ from a plain program's by a relative error of at most 0.00026.
Values sent between devices are 32-bit elements; how exact they have to be, the bound alone decides.
A program may use at most 64 MiB of HBM per device.

v0:
```python
import functools
import math

import jax
import jax.numpy as jnp
from jax import lax
from jax.experimental import pallas as pl
from jax.experimental.pallas import tpu as pltpu
from jax.sharding import PartitionSpec as P

ITERS = 2
SWEEPS = 8


alpha_corner = 0.1
coupling = 0.05


def from_behind(block, axis, distance):
    devices = range(lax.axis_size(axis))
    route = [(i - distance, i) for i in devices if i - distance in devices]
    return lax.ppermute(block, axis, route)


def pad_cube(field):
    widths = [(0, 0)] * (field.ndim - 3) + [(1, 1)] * 3
    return jnp.pad(field, widths)


def neighbours(field):
    padded = pad_cube(field)
    total = padded[..., 2:, 1:-1, 1:-1] + padded[..., :-2, 1:-1, 1:-1]
    total = total + padded[..., 1:-1, 2:, 1:-1] + padded[..., 1:-1, :-2, 1:-1]
    total = total + padded[..., 1:-1, 1:-1, 2:] + padded[..., 1:-1, 1:-1, :-2]
    return total


def complex_times(first, second):
    return jnp.stack(
        [first[0] * second[0] - first[1] * second[1], first[0] * second[1] + first[1] * second[0]]
    )


def relax(spectrum, inverse):
    field = complex_times(inverse, spectrum)
    for repeat in range(SWEEPS - 1):
        field = complex_times(inverse, spectrum + coupling * neighbours(field))
    return field


def inverse_diagonal(angle, absorption, gamma):
    real_part = 1.0 - gamma * jnp.cos(angle) + absorption + 6.0 * coupling
    imag_part = jnp.broadcast_to(gamma * jnp.sin(angle), real_part.shape)
    magnitude = real_part * real_part + imag_part * imag_part
    return jnp.stack([real_part / magnitude, -imag_part / magnitude])


def dft_tables(window_len):
    index = jnp.arange(window_len, dtype=jnp.int32)
    product = index[:, None] * index[None, :] % window_len
    angle = product.astype(jnp.float32) * (2.0 * math.pi / window_len)
    return (jnp.cos(angle), jnp.sin(angle))


def transform_exchange(scaled, window_len):
    pencil = lax.all_to_all(scaled[None], "step", split_axis=1, concat_axis=0, tiled=True)
    cosine, sine = dft_tables(window_len)
    flat = pencil.reshape(window_len, -1)
    real_part = jnp.dot(cosine, flat, precision=lax.Precision.HIGHEST)
    imag_part = -jnp.dot(sine, flat, precision=lax.Precision.HIGHEST)
    shaped = pencil.shape
    spectrum = (
        lax.all_to_all(real_part.reshape(shaped), "step", split_axis=0, concat_axis=1, tiled=True),
        lax.all_to_all(imag_part.reshape(shaped), "step", split_axis=0, concat_axis=1, tiled=True),
    )
    return jnp.stack([spectrum[0][0], spectrum[1][0]])


def untransform_exchange(field, window_len):
    pencil = (
        lax.all_to_all(field[0][None], "step", split_axis=1, concat_axis=0, tiled=True),
        lax.all_to_all(field[1][None], "step", split_axis=1, concat_axis=0, tiled=True),
    )
    cosine, sine = dft_tables(window_len)
    shaped = pencil[0].shape
    values = jnp.dot(cosine, pencil[0].reshape(window_len, -1), precision=lax.Precision.HIGHEST)
    values = values - jnp.dot(
        sine, pencil[1].reshape(window_len, -1), precision=lax.Precision.HIGHEST
    )
    values = values / window_len
    result = lax.all_to_all(values.reshape(shaped), "step", split_axis=0, concat_axis=1, tiled=True)
    return result[0]


def per_device(initial_state, source, absorption):
    window_len = lax.axis_size("step")
    moment = lax.axis_index("step")
    window_index = lax.axis_index("win")
    gamma = alpha_corner ** (1.0 / window_len)
    scale = gamma ** moment.astype(jnp.float32)
    forcing_base = source[0, 0]
    is_first = moment == 0
    state = jnp.zeros_like(forcing_base)
    angle = moment.astype(jnp.float32) * (2.0 * math.pi / window_len)
    inverse = inverse_diagonal(angle, absorption, gamma)
    for repeat in range(ITERS):
        if repeat == 0:
            correction = jnp.where(window_index == 0, initial_state, 0.0)
        else:
            ends = from_behind(state, "step", 1 - window_len)
            before = from_behind(ends, "win", 1)
            before = jnp.where(window_index == 0, initial_state, before)
            correction = before - alpha_corner * ends
        forcing = forcing_base + jnp.where(is_first, correction, 0.0)
        scaled = forcing * scale
        spectrum = transform_exchange(scaled, window_len)
        field = relax(spectrum, inverse)
        values = untransform_exchange(field, window_len)
        state = values / scale
    return state[None, None]


LANES = 128
TILE = 8
GROUP = 8


def tables(length):
    gamma = alpha_corner ** (1.0 / length)
    into, back, angles = [], [], []
    for core in range(2):
        rows_in, rows_back = [], []
        for time in range(length):
            scale = gamma**time
            row_in, row_back = [], []
            for p in range(length // 4):
                j = 2 * p + core
                if j == 0:
                    pair, weight = (1.0, (-1.0) ** time), 1.0 / length
                else:
                    turn = 2.0 * math.pi * (j * time % length) / length
                    pair, weight = (math.cos(turn), -math.sin(turn)), 2.0 / length
                row_in += [value * scale / coupling for value in pair]
                row_back += [value * weight / scale for value in pair]
            rows_in.append(row_in)
            rows_back.append(row_back)
        into.append(rows_in)
        back.append(rows_back)
        angles.append([2.0 * math.pi * (2 * p + core) / length for p in range(length // 4)])
    return into, back, angles


def kernel(
    length, windows, nx, ny, ext, ey,
    source, initial, absorb, out,
    raw, first, absv, coef, base, again, fa, fb, corr,
    psend, pgot, ends, zgot, csend, qsend, qgot, obuf,
    lsem, asend, brecv, fsend, esem, zsem, csem_s, csem_r, qsem_s, qsem_r, osem_s, osem_r,
):
    half = length // 2
    gx, gy = half // 2, 2
    bs, bsy = nx // gx, ny // gy
    reach = SWEEPS - 1
    pairs = length // 4
    units = 2 * pairs
    gamma = alpha_corner ** (1.0 / length)
    into, back, angles = tables(length)
    me = lax.axis_index("step")
    w = lax.axis_index("win")
    core, m = me % 2, me // 2
    partner = m * 2 + (1 - core)
    bx, by = m % gx, m // gx

    def xlo(b):
        if gx == 2:
            return b * (nx - ext)
        return jnp.minimum(jnp.maximum(b * bs - reach, 0), nx - ext)

    def ylo(b):
        return pl.multiple_of(b * (ny - ey), TILE)

    def pick(a, b):
        return jnp.where(core == 0, jnp.float32(a), jnp.float32(b))

    def region(ref, b_x, b_y):
        return ref.at[pl.ds(xlo(b_x), ext), pl.ds(ylo(b_y), ey), :]

    ox = bx * bs - xlo(bx)
    oy = pl.multiple_of(by * bsy - ylo(by), TILE)

    loads = [
        pltpu.make_async_copy(region(absorb, bx, by), absv, lsem.at[0]),
        pltpu.make_async_copy(region(source, bx, by), raw.at[me], lsem.at[1]),
        pltpu.make_async_copy(region(initial, bx, by), first, lsem.at[2]),
    ]
    for load in loads:
        load.start()
    zero_row = jnp.zeros((ey, LANES), jnp.float32)
    for u in range(units):
        for ref in (fa, fb):
            ref[u, 0, pl.ds(TILE, ey)] = zero_row
            ref[u, ext + 1, pl.ds(TILE, ey)] = zero_row
            for r in range(1, ext + 1):
                ref[u, r, pl.ds(0, TILE)] = zero_row[:TILE]
                ref[u, r, pl.ds(TILE + ey, TILE)] = zero_row[:TILE]
    if gx > 2:
        corr[...] = jnp.zeros_like(corr)

    barrier = pltpu.get_barrier_semaphore()
    for d in range(1, length):
        pl.semaphore_signal(
            barrier, inc=1, device_id={"step": (me + d) % length}, device_id_type=pl.DeviceIdType.MESH
        )

    @pl.when(w > 0)
    def _():
        pl.semaphore_signal(barrier, inc=1, device_id={"win": w - 1}, device_id_type=pl.DeviceIdType.MESH)

    @pl.when(w < windows - 1)
    def _():
        pl.semaphore_signal(barrier, inc=1, device_id={"win": w + 1}, device_id_type=pl.DeviceIdType.MESH)

    nearby = jnp.where(w > 0, 1, 0) + jnp.where(w < windows - 1, 1, 0)
    pl.semaphore_wait(barrier, length - 1 + nearby)

    def remote(src, dst, send, recv, **where):
        return pltpu.make_async_remote_copy(
            src_ref=src, dst_ref=dst, send_sem=send, recv_sem=recv,
            device_id=where, device_id_type=pl.DeviceIdType.MESH,
        )

    outgoing = []
    for d in range(1, half):
        to = (m + d) % half
        copy = remote(
            region(source, to % gx, to // gx), raw.at[me], asend.at[d], brecv.at[me], step=to * 2 + core
        )
        copy.start()
        outgoing.append(copy)
    copy = remote(region(source, bx, by), raw.at[me], asend.at[0], brecv.at[me], step=partner)
    copy.start()
    outgoing.append(copy)

    def grouped(begin, count, work, most=GROUP):
        size = -(-count // max(1, count // most))

        def body(g, carry):
            work(begin + g * size, size)
            return carry

        lax.fori_loop(0, count // size, body, 0)
        if count % size:
            work(begin + count - size, size)

    def each(one):
        def work(start, rows):
            for n in range(rows):
                one(start + n)

        return work

    loads[0].wait()

    def coefficients(i):
        for p in range(pairs):
            rows = absv[i]
            cosine = pick(math.cos(angles[0][p]), math.cos(angles[1][p]))
            imag = pick(gamma * math.sin(angles[0][p]), gamma * math.sin(angles[1][p]))
            real = 1.0 - gamma * cosine + rows + 6.0 * coupling
            over = coupling / (real * real + imag * imag)
            coef[3 * p, i] = real * over
            coef[3 * p + 1, i] = -imag * over
            if p == 0:
                other = pick(-1.0, math.cos(angles[1][p]))
                real = 1.0 - gamma * other + rows + 6.0 * coupling
                over = coupling / (real * real + imag * imag)
                coef[3 * p + 2, i] = real * over

    grouped(0, ext, each(coefficients))

    def weights(p, i):
        straight = coef[3 * p, i]
        return straight, (coef[3 * p + 2, i] if p == 0 else straight), coef[3 * p + 1, i]

    def arrival(t):
        return remote(raw.at[t], raw.at[t], asend.at[0], brecv.at[t], step=partner)

    for d in range(1, half):
        t = ((m + half - d) % half) * 2 + core
        arrival(t).wait_recv()
        copy = remote(raw.at[t], raw.at[t], fsend.at[d], brecv.at[t], step=partner)
        copy.start()
        outgoing.append(copy)
    for d in range(half):
        arrival(((m + half - d) % half) * 2 + (1 - core)).wait_recv()
    loads[1].wait()
    loads[2].wait()
    is_first = jnp.where(w == 0, jnp.float32(1.0 / coupling), jnp.float32(0.0))

    def second_weight(p, weight):
        return weight[2] + (pick(1.0, 0.0) * weight[1] if p == 0 else 0.0)

    def transform(i):
        begin = first[i] * is_first
        fields = [raw[t, i] for t in range(length)]
        for p in range(pairs):
            weight = weights(p, i)
            s0, s1 = begin, begin * pick(1.0, 0.0) if p == 0 else None
            for t in range(length):
                s0 = s0 + pick(into[0][t][2 * p], into[1][t][2 * p]) * fields[t]
                term = pick(into[0][t][2 * p + 1], into[1][t][2 * p + 1]) * fields[t]
                s1 = term if s1 is None else s1 + term
            b0 = weight[0] * s0 - weight[2] * s1
            b1 = weight[1] * s1 + weight[2] * s0
            base[2 * p, i] = b0
            base[2 * p + 1, i] = b1
            fa[2 * p, i + 1, pl.ds(TILE, ey)] = b0
            fa[2 * p + 1, i + 1, pl.ds(TILE, ey)] = b1

    grouped(0, ext, each(transform), GROUP // 2)

    lane = lax.broadcasted_iota(jnp.int32, (ey, LANES), 1)

    def around(ref, u, r):
        v = ref[u, r, pl.ds(TILE, ey)]
        total = jnp.where(lane == 0, 0.0, pltpu.roll(v, 1, 1))
        total = total + jnp.where(lane == LANES - 1, 0.0, pltpu.roll(v, LANES - 1, 1))
        beside = ref[u, r - 1, pl.ds(TILE, ey)] + ref[u, r + 1, pl.ds(TILE, ey)]
        return total + (beside + (ref[u, r, pl.ds(TILE - 1, ey)] + ref[u, r, pl.ds(TILE + 1, ey)]))

    def sweep_rows(base, here, there, start, rows):
        for n in range(rows):
            i = start + n
            for p in range(pairs):
                weight = weights(p, i)
                n0 = around(here, 2 * p, i + 1)
                n1 = around(here, 2 * p + 1, i + 1)
                there[2 * p, i + 1, pl.ds(TILE, ey)] = base[2 * p, i] + (weight[0] * n0 - weight[2] * n1)
                there[2 * p + 1, i + 1, pl.ds(TILE, ey)] = base[2 * p + 1, i] + (
                    weight[1] * n1 + weight[2] * n0
                )

    def sweeps(base):
        here, there = fa, fb
        for k in range(1, SWEEPS):
            begin, count = (bx * k, ext - k) if gx == 2 else (0, ext)
            grouped(begin, count, functools.partial(sweep_rows, base, here, there))
            here, there = there, here
        return here

    final = sweeps(base)

    def part(t, y0, rows):
        total = None
        for u in range(units):
            factor = pick(back[0][t[0]][u], back[1][t[1]][u])
            term = factor * final[u, pl.ds(ox + 1, bs), pl.ds(y0 + TILE, rows), :]
            total = term if total is None else total + term
        return total

    last = (length - 1, length - 1)
    psend[...] = part(last, pl.multiple_of(oy + TILE * (1 - core), TILE), TILE)
    swap = remote(psend, pgot, esem.at[0], esem.at[1], step=partner)
    swap.start()
    mine = part(last, pl.multiple_of(oy + TILE * core, TILE), TILE)
    swap.wait_recv()
    mine = mine + pgot[...]
    ends[...] = mine
    outgoing.append(swap)

    onward = remote(ends, zgot, zsem.at[0], zsem.at[1], win=(w + 1) % windows)

    @pl.when(w < windows - 1)
    def _():
        onward.start()

    @pl.when(w == 0)
    def _():
        zgot[...] = jnp.zeros_like(zgot)

    @pl.when(w > 0)
    def _():
        onward.wait_recv()

    change = zgot[...] - alpha_corner * ends[...]
    csend[...] = change
    corr[pl.ds(ox, bs), pl.ds(pl.multiple_of(oy + TILE * core, TILE), TILE), :] = change

    def spread(ex, ey_, send):
        rows, skip = (bs, 0) if ex == 0 else (reach, bs - reach if ex == 1 else 0)
        tx, ty = (bx + ex, by + ey_) if send else (bx, by)
        fx, fy = (bx, by) if send else (bx - ex, by - ey_)
        ax, ay = (tx, ty) if send else (fx, fy)
        inside = (ax >= 0) & (ax < gx) & (ay >= 0) & (ay < gy)
        slot = ((ex + 1) * 3 + (ey_ + 1)) * 2
        for c in range(2):
            near = c == (1 if ey_ == 1 else 0)
            if send:
                okay = inside if ey_ == 0 else inside & (core == (1 if ey_ == 1 else 0))
                if ex == 0 and ey_ == 0:
                    okay = core != c
                fc, tc = core, c
            else:
                if ey_ != 0 and not near:
                    continue
                okay = inside
                if ex == 0 and ey_ == 0:
                    okay = core != c
                fc, tc = c, core

            @pl.when(okay)
            def _(c=c, fc=fc, tc=tc):
                copy = remote(
                    csend.at[pl.ds(skip, rows)],
                    corr.at[
                        pl.ds(fx * bs + skip - xlo(tx), rows),
                        pl.ds(pl.multiple_of(fy * bsy + TILE * fc - ylo(ty), TILE), TILE),
                        :,
                    ],
                    csem_s.at[slot + c],
                    csem_r.at[slot + fc],
                    step=(ty * gx + tx) * 2 + tc if send == 1 else partner,
                )
                if send == 1:
                    copy.start()
                elif send == 2:
                    copy.wait_send()
                else:
                    copy.wait_recv()

    offsets = [(ex, e) for ex in (-1, 0, 1) for e in (-1, 0, 1)]
    for ex, e in offsets:
        spread(ex, e, 1)
    for ex, e in offsets:
        spread(ex, e, 0)

    def correct(i):
        x = corr[i] * (1.0 / coupling)
        for p in range(pairs):
            weight = weights(p, i)
            b0 = base[2 * p, i] + weight[0] * x
            b1 = base[2 * p + 1, i] + second_weight(p, weight) * x
            again[2 * p, i] = b0
            again[2 * p + 1, i] = b1
            fa[2 * p, i + 1, pl.ds(TILE, ey)] = b0
            fa[2 * p + 1, i + 1, pl.ds(TILE, ey)] = b1

    grouped(0, ext, each(correct))
    final = sweeps(again)

    for k in range(half):
        qsend[k] = part((2 * k + 1, 2 * k), oy, bsy)
        copy = remote(qsend.at[k], qgot.at[k], qsem_s.at[k], qsem_r.at[k], step=partner)
        copy.start()
        outgoing.append(copy)
    for k in range(half):
        obuf[k] = part((2 * k, 2 * k + 1), oy, bsy)

    def place(b_x, b_y):
        return out.at[pl.ds(b_x * bs, bs), pl.ds(pl.multiple_of(b_y * bsy, TILE), bsy), :]

    for k in range(half):
        remote(qsend.at[k], qgot.at[k], qsem_s.at[k], qsem_r.at[k], step=partner).wait_recv()
        obuf[k] = obuf[k] + qgot[k]

        @pl.when(m == k)
        def _(k=k):
            pltpu.make_async_copy(obuf.at[k], place(bx, by), lsem.at[3]).start()

        @pl.when(m != k)
        def _(k=k):
            remote(obuf.at[k], place(bx, by), osem_s.at[k], osem_r.at[m], step=2 * k + core).start()

    for copy in outgoing:
        copy.wait_send()
    for ex, e in offsets:
        spread(ex, e, 2)

    @pl.when(w < windows - 1)
    def _():
        onward.wait_send()

    for k in range(half):

        @pl.when(m == k)
        def _(k=k):
            pltpu.make_async_copy(obuf.at[k], place(bx, by), lsem.at[3]).wait()

        @pl.when(m != k)
        def _(k=k):
            done = remote(obuf.at[k], place(k % gx, k // gx), osem_s.at[k], osem_r.at[k], step=partner)
            done.wait_send()
            done.wait_recv()


def blocks(initial_state, source, absorption):
    length = lax.axis_size("step")
    windows = lax.axis_size("win")
    nx, ny, nz = initial_state.shape
    half = length // 2
    gx, reach = half // 2, SWEEPS - 1
    bs, bsy = nx // gx, ny // 2
    ext = min(nx, bs + reach * (1 if gx == 2 else 2))
    ey = bsy + -(-reach // TILE) * TILE
    units = length // 2
    f32 = jnp.float32
    dma = pltpu.SemaphoreType.DMA
    return pl.pallas_call(
        functools.partial(kernel, length, windows, nx, ny, ext, ey),
        out_shape=jax.ShapeDtypeStruct((nx, ny, nz), f32),
        in_specs=[pl.BlockSpec(memory_space=pl.ANY)] * 3,
        out_specs=pl.BlockSpec(memory_space=pl.ANY),
        scratch_shapes=[
            pltpu.VMEM((length, ext, ey, nz), f32),
            pltpu.VMEM((ext, ey, nz), f32),
            pltpu.VMEM((ext, ey, nz), f32),
            pltpu.VMEM((3 * length // 4, ext, ey, nz), f32),
            pltpu.VMEM((units, ext, ey, nz), f32),
            pltpu.VMEM((units, ext, ey, nz), f32),
            pltpu.VMEM((units, ext + 2, ey + 2 * TILE, nz), f32),
            pltpu.VMEM((units, ext + 2, ey + 2 * TILE, nz), f32),
            pltpu.VMEM((ext, ey, nz), f32),
            pltpu.VMEM((bs, TILE, nz), f32),
            pltpu.VMEM((bs, TILE, nz), f32),
            pltpu.VMEM((bs, TILE, nz), f32),
            pltpu.VMEM((bs, TILE, nz), f32),
            pltpu.VMEM((bs, TILE, nz), f32),
            pltpu.VMEM((half, bs, bsy, nz), f32),
            pltpu.VMEM((half, bs, bsy, nz), f32),
            pltpu.VMEM((half, bs, bsy, nz), f32),
            dma((4,)),
            dma((half,)),
            dma((length,)),
            dma((half,)),
            dma((2,)),
            dma((2,)),
            dma((18,)),
            dma((18,)),
            dma((half,)),
            dma((half,)),
            dma((half,)),
            dma((half,)),
        ],
        compiler_params=pltpu.CompilerParams(
            collective_id=0, has_side_effects=True, vmem_limit_bytes=28 * 1024 * 1024
        ),
    )(source[0, 0], initial_state, absorption)[None, None]


def fits(mesh, shape):
    length = mesh.shape["step"]
    if length % 8 or shape[2] != LANES or shape[1] != 4 * TILE:
        return False
    gx = length // 4
    return shape[0] % gx == 0 and shape[0] // gx >= SWEEPS - 1


def solution(mesh):
    def body(initial_state, source, absorption):
        plan = blocks if fits(mesh, initial_state.shape) else per_device
        return plan(initial_state, source, absorption)

    return jax.shard_map(
        body,
        mesh=mesh,
        in_specs=(P(), P("win", "step", None, None, None), P()),
        out_specs=P("win", "step", None, None, None),
        check_vma=False,
    )
```

profile of v0, /device:TPU:12, one launch (start us, length us, event | category | flops | bytes accessed | tf_op | source)
XLA Modules:
  0.0 49.6 jit_solution(10076711884944219785)
XLA Ops:
  0.0 0.0 copy-start
  0.0 1.0 %copy-done = f32[1,1,32,32,128]{4,3,2,1,0:T(8,128)S(1)} copy-done((f32[1,1,32,32,128]{4,3,2,1,0:T(8,128)S(1)}, f32[1,1,32,32,128]{4,3,2,1,0:T(8,128)}, u32[]{:S(2)}) %copy-start) | copy-done | bytes 524312
  1.0 0.0 copy-start.1
  1.0 1.0 %copy-done.1 = f32[32,32,128]{2,1,0:T(8,128)S(1)} copy-done((f32[32,32,128]{2,1,0:T(8,128)S(1)}, f32[32,32,128]{2,1,0:T(8,128)}, u32[]{:S(2)}) %copy-start.1) | copy-done | bytes 524312
  2.1 0.0 copy-start.2
  2.1 1.0 %copy-done.2 = f32[32,32,128]{2,1,0:T(8,128)S(1)} copy-done((f32[32,32,128]{2,1,0:T(8,128)S(1)}, f32[32,32,128]{2,1,0:T(8,128)}, u32[]{:S(2)}) %copy-start.2) | copy-done | bytes 524312
  3.1 45.6 %shard_map.37 = f32[32,32,128]{2,1,0:T(8,128)S(1)} custom-call(f32[32,32,128]{2,1,0:T(8,128)S(1)} %bitcast.3, f32[32,32,128]{2,1,0:T(8,128)S(1)} %copy-done.1, f32[32,32,128]{2,1,0:T(8,128)S(1)} %copy-done.2), custom_call_target="tpu_custom_call" | custom-call | tf_op jit(solution)/shard_map/pallas_call | solution.py:508
  48.8 0.8 %copy.5 = f32[1,1,32,32,128]{4,3,2,1,0:T(8,128)} copy(f32[1,1,32,32,128]{4,3,2,1,0:T(8,128)S(1)} %bitcast.2) | data formatting | bytes 1048576
Async XLA Ops:
  0.0 1.0 %copy-start = (f32[1,1,32,32,128]{4,3,2,1,0:T(8,128)S(1)}, f32[1,1,32,32,128]{4,3,2,1,0:T(8,128)}, u32[]{:S(2)}) copy-start(f32[1,1,32,32,128]{4,3,2,1,0:T(8,128)} %param.4) | copy-start | bytes 1572868
  1.0 1.0 %copy-start.1 = (f32[32,32,128]{2,1,0:T(8,128)S(1)}, f32[32,32,128]{2,1,0:T(8,128)}, u32[]{:S(2)}) copy-start(f32[32,32,128]{2,1,0:T(8,128)} %initial.1) | copy-start | bytes 1572868
  2.1 1.0 %copy-start.2 = (f32[32,32,128]{2,1,0:T(8,128)S(1)}, f32[32,32,128]{2,1,0:T(8,128)}, u32[]{:S(2)}) copy-start(f32[32,32,128]{2,1,0:T(8,128)} %absorb.1) | copy-start | bytes 1572868
where the time goes:
time: 49.8 us; the launch traced here: 49.6 us
  Pallas kernels  45.6 us (92%)
  local copies, waits for them, and re-layouts  3.92 us (8%)
    pallas_call x1, Pallas kernels, blocks(): pl.pallas_call(functools.partial(kernel, length, windows, nx, ny, ext, ey...  45.6 us
    unnamed x7, local copies, waits for them, and re-layouts  3.92 us

commit v1 on v0

--- a/solution.py
+++ b/solution.py
@@ -547,6 +547,563 @@
     )(source[0, 0], initial_state, absorption)[None, None]
 
 
+def spans(ext, bs, reach):
+    bounds = [0, *range(reach + 5, ext, 4), ext]
+    arrive = list(zip(bounds[:-1], bounds[1:]))
+    final = [(max(0, a - reach), b - reach) for a, b in arrive]
+    second = [(a, b, "own", e) for e, (a, b) in enumerate(final)]
+    for e in reversed(range(len(final))):
+        a, b = final[e]
+        if b > bs - reach:
+            a = max(a, bs - reach)
+            second.append((2 * bs - b, 2 * bs - a, "beyond", e))
+    leave = [(max(0, a - reach), b - reach) for a, b, _, _ in second if b > reach]
+    return arrive, final, second, leave
+
+
+def wave_kernel(
+    length, windows, nx, ny, ext, ey, plan,
+    source, initial, absorb, out,
+    srcv, raw, first, absv, coef, level, fin, corr,
+    emine, esend, egot, zgot, zother, csend, xsend, xgot, obuf,
+    lsem, asend, brecv, fsend, esem_s, esem_r, zsem_s, zsem_r, csem_s, csem_r, xsem_s, xsem_r, osem_s, osem_r, hsem,
+):
+    arrive, final, second, leave = plan
+    half = length // 2
+    bs, bsy = nx // 2, ny // 2
+    reach = SWEEPS - 1
+    pairs = length // 4
+    units = 2 * pairs
+    kept = half // 2
+    gamma = alpha_corner ** (1.0 / length)
+    into, back, angles = tables(length)
+    me = lax.axis_index("step")
+    w = lax.axis_index("win")
+    core, m = me % 2, me // 2
+    partner = m * 2 + (1 - core)
+    bx, by = m % 2, m // 2
+    near = core == 1 - by
+
+    def chip(b_x, b_y):
+        return b_y * 2 + b_x
+
+    def xlo(b):
+        return b * (nx - ext)
+
+    def ylo(b):
+        return pl.multiple_of(b * (ny - ey), TILE)
+
+    def rows_of(lo, hi, b=bx):
+        return lo + b * (ext - lo - hi)
+
+    def own_of(lo, hi, b=bx):
+        return lo + b * (bs - lo - hi)
+
+    def pick(a, b):
+        if a == b:
+            return jnp.float32(a)
+        return jnp.where(core == 0, jnp.float32(a), jnp.float32(b))
+
+    def region(ref, b_x, b_y, lo, hi):
+        rows = pl.ds(xlo(b_x) + rows_of(lo, hi, b_x), hi - lo)
+        return ref.at[rows, pl.ds(ylo(b_y), ey), :]
+
+    ox = bx * bs - xlo(bx)
+    oy = pl.multiple_of(by * bsy - ylo(by), TILE)
+
+    loads = [
+        pltpu.make_async_copy(source, srcv, lsem.at[0]),
+        pltpu.make_async_copy(region(absorb, bx, by, 0, ext), absv, lsem.at[1]),
+        pltpu.make_async_copy(region(source, bx, by, 0, ext), raw.at[me], lsem.at[2]),
+        pltpu.make_async_copy(region(initial, bx, by, 0, ext), first, lsem.at[3]),
+    ]
+    for load in loads:
+        load.start()
+
+    barrier = pltpu.get_barrier_semaphore()
+
+    def greet(**where):
+        pl.semaphore_signal(barrier, inc=1, device_id=where, device_id_type=pl.DeviceIdType.MESH)
+
+    for d in range(1, length):
+        greet(step=(me + d) % length)
+
+    @pl.when(w > 0)
+    def _():
+        greet(win=w - 1, step=me)
+        greet(win=w - 1, step=partner)
+
+    @pl.when(w < windows - 1)
+    def _():
+        greet(win=w + 1, step=me)
+        greet(win=w + 1, step=partner)
+
+    @pl.when(w == 0)
+    def _():
+        zgot[...] = jnp.zeros_like(zgot)
+        zother[...] = jnp.zeros_like(zother)
+
+    nearby = jnp.where(w > 0, 2, 0) + jnp.where(w < windows - 1, 2, 0)
+    loads[0].wait()
+    pl.semaphore_wait(barrier, length - 1 + nearby)
+
+    def remote(src, dst, send, recv, **where):
+        return pltpu.make_async_remote_copy(
+            src_ref=src, dst_ref=dst, send_sem=send, recv_sem=recv,
+            device_id=where, device_id_type=pl.DeviceIdType.MESH,
+        )
+
+    outgoing = []
+
+    def launch(copy):
+        copy.start()
+        outgoing.append(copy)
+
+    others = [(1, 1), (1, 0), (0, 1)]
+
+    def beside(ex, e_y):
+        return (bx + ex) % 2, (by + e_y) % 2
+
+    for c, (lo, hi) in enumerate(arrive):
+        for d, (ex, e_y) in enumerate(others):
+            tx, ty = beside(ex, e_y)
+            launch(
+                remote(
+                    region(srcv, tx, ty, lo, hi),
+                    raw.at[me, pl.ds(rows_of(lo, hi, tx), hi - lo)],
+                    asend.at[d, c], brecv.at[me, c], step=chip(tx, ty) * 2 + core,
+                )
+            )
+        here = pl.ds(rows_of(lo, hi), hi - lo)
+        launch(
+            remote(
+                region(srcv, bx, by, lo, hi), raw.at[me, here],
+                asend.at[len(others), c], brecv.at[me, c], step=partner,
+            )
+        )
+
+    zero_row = jnp.zeros((ey, LANES), jnp.float32)
+
+    def rim(g, carry):
+        k, u = g // units, g % units
+        for r in (0, ext + 1):
+            level[k, u, r, pl.ds(TILE, ey)] = zero_row
+        for r in range(1, ext + 1):
+            level[k, u, r, pl.ds(0, TILE)] = zero_row[:TILE]
+            level[k, u, r, pl.ds(TILE + ey, TILE)] = zero_row[:TILE]
+        return carry
+
+    lax.fori_loop(0, reach * units, rim, 0)
+
+    def grouped(begin, count, work, most):
+        groups = -(-count // most)
+        size = -(-count // groups)
+        if groups == 1:
+            work(begin, count)
+            return
+
+        def body(g, carry):
+            work(begin + g * size, size)
+            return carry
+
+        lax.fori_loop(0, count // size, body, 0)
+        if count % size:
+            work(begin + count - count % size, count % size)
+
+    loads[1].wait()
+
+    def coefficients(start, rows):
+        for n in range(rows):
+            i = start + n
+            for p in range(pairs):
+                here = absv[i]
+                cosine = pick(math.cos(angles[0][p]), math.cos(angles[1][p]))
+                imag = pick(gamma * math.sin(angles[0][p]), gamma * math.sin(angles[1][p]))
+                real = 1.0 - gamma * cosine + here + 6.0 * coupling
+                over = coupling / (real * real + imag * imag)
+                coef[3 * p, i] = real * over
+                coef[3 * p + 1, i] = -imag * over
+                if p == 0:
+                    other = pick(-1.0, math.cos(angles[1][p]))
+                    real = 1.0 - gamma * other + here + 6.0 * coupling
+                    over = coupling / (real * real + imag * imag)
+                    coef[3 * p + 2, i] = real * over
+
+    grouped(0, ext, coefficients, 4)
+
+    def weights(p, i, y0=0, rows=ey):
+        part = pl.ds(y0, rows)
+        straight = coef[3 * p, i, part]
+        return straight, (coef[3 * p + 2, i, part] if p == 0 else straight), coef[3 * p + 1, i, part]
+
+    is_first = jnp.where(w == 0, jnp.float32(1.0 / coupling), jnp.float32(0.0))
+
+    def combine(pair, values):
+        total = None
+        for (a, b), value in zip(pair, values):
+            if a == 0 and b == 0:
+                continue
+            term = value if a == 1 and b == 1 else pick(a, b) * value
+            total = term if total is None else total + term
+        return total
+
+    def spectrum(start, rows):
+        for n in range(rows):
+            i = start + n
+            folded = []
+            for t in range(half):
+                early, late = gamma**t / coupling, gamma ** (t + half) / coupling
+                folded.append(early * raw[t, i] + pick(late, -late) * raw[t + half, i])
+            folded[0] = folded[0] + first[i] * is_first
+            for p in range(pairs):
+                weight = weights(p, i)
+                turn = [
+                    [
+                        tuple(into[c][t][2 * p + q] * coupling / gamma**t for c in range(2))
+                        for t in range(half)
+                    ]
+                    for q in range(2)
+                ]
+                turn = [[tuple(round(v, 15) for v in pair) for pair in row] for row in turn]
+                s0 = combine(turn[0], folded)
+                s1 = combine(turn[1], folded)
+                level[0, 2 * p, i + 1, pl.ds(TILE, ey)] = weight[0] * s0 - weight[2] * s1
+                level[0, 2 * p + 1, i + 1, pl.ds(TILE, ey)] = weight[1] * s1 + weight[2] * s0
+
+    def stencil(k, u, start, rows, y0, depth):
+        lane = lax.broadcasted_iota(jnp.int32, (depth, LANES), 1)
+        at = pl.multiple_of(y0 + TILE, TILE)
+        line = [level[k, u, start + n, pl.ds(at, depth)] for n in range(rows + 2)]
+        sums = []
+        for n in range(1, rows + 1):
+            v = line[n]
+            around = level.at[k, u, start + n, pl.ds(y0, depth + 2 * TILE), :]
+            total = jnp.where(lane == 0, 0.0, pltpu.roll(v, 1, 1))
+            total = total + jnp.where(lane == LANES - 1, 0.0, pltpu.roll(v, LANES - 1, 1))
+            across = around[pl.ds(TILE - 1, depth)] + around[pl.ds(TILE + 1, depth)]
+            sums.append(total + ((line[n - 1] + line[n + 1]) + across))
+        return sums
+
+    def sweep_rows(k, start, rows):
+        last = k == reach
+        y0, depth = (oy, bsy) if last else (0, ey)
+        at = pl.multiple_of(y0 + TILE, TILE)
+        for p in range(pairs):
+            s0 = stencil(k - 1, 2 * p, start, rows, y0, depth)
+            s1 = stencil(k - 1, 2 * p + 1, start, rows, y0, depth)
+            for n in range(rows):
+                i = start + n
+                weight = weights(p, i, y0, depth)
+                b0 = level[0, 2 * p, i + 1, pl.ds(at, depth)]
+                b1 = level[0, 2 * p + 1, i + 1, pl.ds(at, depth)]
+                v0 = b0 + (weight[0] * s0[n] - weight[2] * s1[n])
+                v1 = b1 + (weight[1] * s1[n] + weight[2] * s0[n])
+                if last:
+                    fin[2 * p, i - ox] = v0
+                    fin[2 * p + 1, i - ox] = v1
+                else:
+                    level[k, 2 * p, i + 1, pl.ds(TILE, ey)] = v0
+                    level[k, 2 * p + 1, i + 1, pl.ds(TILE, ey)] = v1
+
+    def sweeps(a, b):
+        for k in range(1, SWEEPS):
+            lo, hi = max(0, a - k), b - k
+            if hi > lo:
+                grouped(rows_of(lo, hi), hi - lo, functools.partial(sweep_rows, k), 6)
+
+    def part(t, start, rows, y0, depth):
+        total = None
+        for u in range(units):
+            factor = pick(back[0][t[0]][u], back[1][t[1]][u])
+            term = factor * fin[u, pl.ds(start, rows), pl.ds(y0, depth), :]
+            total = term if total is None else total + term
+        return total
+
+    def strip(ref, lo, hi):
+        return ref.at[pl.ds(own_of(lo, hi), hi - lo)]
+
+    def swap(e):
+        lo, hi = final[e]
+        return remote(strip(esend, lo, hi), strip(egot, lo, hi), esem_s.at[e], esem_r.at[e], step=partner)
+
+    def onward(e):
+        lo, hi = final[e]
+        after = (w + 1) % windows
+        return [
+            remote(
+                strip(emine, lo, hi), strip(zgot, lo, hi),
+                zsem_s.at[0, e], zsem_r.at[0, e], win=after, step=me,
+            ),
+            remote(
+                strip(esend, lo, hi), strip(zother, lo, hi),
+                zsem_s.at[1, e], zsem_r.at[1, e], win=after, step=partner,
+            ),
+        ]
+
+    def finish(e):
+        lo, hi = final[e]
+        last = (length - 1, length - 1)
+        start, rows = own_of(lo, hi), hi - lo
+        esend[pl.ds(start, rows)] = part(last, start, rows, pl.multiple_of(TILE * (1 - core), TILE), TILE)
+        emine[pl.ds(start, rows)] = part(last, start, rows, pl.multiple_of(TILE * core, TILE), TILE)
+        launch(swap(e))
+
+        @pl.when(w < windows - 1)
+        def _():
+            for copy in onward(e):
+                copy.start()
+
+    def landing(f_x, f_y, f_c, t_x, t_y, lo, hi):
+        rows = pl.ds(f_x * bs + own_of(lo, hi, f_x) - xlo(t_x), hi - lo)
+        depth = pl.ds(pl.multiple_of(f_y * bsy + TILE * f_c - ylo(t_y), TILE), TILE)
+        return corr.at[rows, depth, :]
+
+    def edge(e):
+        lo, hi = final[e]
+        return max(lo, bs - reach), hi
+
+    def spread(e, act):
+        lo, hi = final[e]
+
+        def one(slot, where, to_core, lo, hi, recv):
+            tx, ty = beside(*where)
+            act(
+                remote(
+                    strip(csend, lo, hi), landing(bx, by, core, tx, ty, lo, hi),
+                    csem_s.at[slot, e], csem_r.at[recv, e], step=chip(tx, ty) * 2 + to_core,
+                )
+            )
+
+        lo2, hi2 = edge(e)
+        if hi2 > lo2:
+
+            @pl.when(near)
+            def _():
+                for c in range(2):
+                    one(1 + c, (1, 1), c, lo2, hi2, 4)
+
+            for c in range(2):
+                one(3 + c, (1, 0), c, lo2, hi2, 2 + core)
+
+        @pl.when(near)
+        def _():
+            for c in range(2):
+                one(5 + c, (0, 1), c, lo, hi, 1)
+
+        one(0, (0, 0), 1 - core, lo, hi, 0)
+
+    def gather(e, kind):
+        lo, hi = final[e]
+        if kind == "own":
+            sources = [(0, (0, 0), 1 - core), (1, (0, 1), by)]
+        else:
+            lo, hi = edge(e)
+            sources = [(2, (1, 0), 0), (3, (1, 0), 1), (4, (1, 1), by)]
+        for slot, where, f_c in sources:
+            fx, fy = beside(*where)
+            remote(
+                strip(csend, lo, hi), landing(fx, fy, f_c, bx, by, lo, hi),
+                csem_s.at[0, e], csem_r.at[slot, e], step=partner,
+            ).wait_recv()
+
+    def change(e):
+        lo, hi = final[e]
+        swap(e).wait_recv()
+
+        @pl.when(w > 0)
+        def _():
+            for copy in onward(e):
+                copy.wait_recv()
+
+        mine = pl.ds(own_of(lo, hi), hi - lo)
+        value = (zgot[mine] + zother[mine]) - alpha_corner * (emine[mine] + egot[mine])
+        csend[mine] = value
+        corr[pl.ds(ox + own_of(lo, hi), hi - lo), pl.ds(pl.multiple_of(oy + TILE * core, TILE), TILE), :] = value
+        spread(e, lambda copy: copy.start())
+
+    def arrival(t, c):
+        lo, hi = arrive[c]
+        return raw.at[t, pl.ds(rows_of(lo, hi), hi - lo)]
+
+    for c, (a, b) in enumerate(arrive):
+        for d, (ex, e_y) in enumerate(others):
+            t = chip(*beside(ex, e_y)) * 2 + core
+            block = arrival(t, c)
+            copy = remote(block, block, fsend.at[d, c], brecv.at[t, c], step=partner)
+            copy.wait_recv()
+            launch(copy)
+        if c == 0:
+            loads[2].wait()
+            loads[3].wait()
+        for ex, e_y in [(0, 0), *others]:
+            t = chip(*beside(ex, e_y)) * 2 + (1 - core)
+            block = arrival(t, c)
+            remote(block, block, fsend.at[0, c], brecv.at[t, c], step=partner).wait_recv()
+        grouped(rows_of(a, b), b - a, spectrum, 3)
+        sweeps(a, b)
+        finish(c)
+        if c:
+            change(c - 1)
+
+    def second_weight(p, weight):
+        return weight[2] + (pick(1.0, 0.0) * weight[1] if p == 0 else 0.0)
+
+    def correct(start, rows):
+        for n in range(rows):
+            i = start + n
+            x = corr[i] * (1.0 / coupling)
+            for p in range(pairs):
+                weight = weights(p, i)
+                spot = pl.ds(TILE, ey)
+                level[0, 2 * p, i + 1, spot] = level[0, 2 * p, i + 1, spot] + weight[0] * x
+                level[0, 2 * p + 1, i + 1, spot] = (
+                    level[0, 2 * p + 1, i + 1, spot] + second_weight(p, weight) * x
+                )
+
+    def trade(i, o):
+        lo, hi = leave[o]
+        mine = pl.ds(own_of(lo, hi), hi - lo)
+        return remote(xsend.at[i, mine], xgot.at[i, mine], xsem_s.at[i, o], xsem_r.at[i, o], step=partner)
+
+    def emit(o):
+        lo, hi = leave[o]
+        start, rows = own_of(lo, hi), hi - lo
+        for i in range(kept):
+            xsend[i, pl.ds(start, rows)] = part((2 * i + 1, 2 * i), start, rows, 0, bsy)
+            launch(trade(i, o))
+        for i in range(kept):
+            obuf[i, pl.ds(start, rows)] = part((2 * i, 2 * i + 1), start, rows, 0, bsy)
+
+    def place(b_x, b_y, lo, hi):
+        rows = pl.ds(b_x * bs + own_of(lo, hi, b_x), hi - lo)
+        return out.at[rows, pl.ds(pl.multiple_of(b_y * bsy, TILE), bsy), :]
+
+    def stay(k, o):
+        lo, hi = leave[o]
+        return pltpu.make_async_copy(strip(obuf.at[k], lo, hi), place(bx, by, lo, hi), hsem.at[o])
+
+    def deliver(k, o, b_x, b_y, slot):
+        lo, hi = leave[o]
+        return remote(
+            strip(obuf.at[k], lo, hi), place(b_x, b_y, lo, hi),
+            osem_s.at[k, o], osem_r.at[slot, o], step=2 * k + core,
+        )
+
+    ratio = gamma ** (-half)
+
+    def settle(o):
+        lo, hi = leave[o]
+        mine = pl.ds(own_of(lo, hi), hi - lo)
+        for i in range(kept):
+            trade(i, o).wait_recv()
+            ours, theirs = obuf[i, mine], xgot[i, mine]
+            obuf[i, mine] = ours + theirs
+            obuf[i + kept, mine] = pick(ratio, -ratio) * (ours - theirs)
+            for k in (i, i + kept):
+
+                @pl.when(m == k)
+                def _(k=k):
+                    stay(k, o).start()
+
+                @pl.when(m != k)
+                def _(k=k):
+                    deliver(k, o, bx, by, m).start()
+
+    pending = len(final) - 1
+    o = -1
+    for g, (a, b, kind, e) in enumerate(second):
+        if kind == "own" and e == pending - 1:
+            change(pending)
+        gather(e, kind)
+        grouped(rows_of(a, b), b - a, correct, 5)
+        sweeps(a, b)
+        if b > reach:
+            o += 1
+            emit(o)
+            if o:
+                settle(o - 1)
+    settle(o)
+
+    for copy in outgoing:
+        copy.wait_send()
+    for e in range(len(final)):
+        spread(e, lambda copy: copy.wait_send())
+
+    @pl.when(w < windows - 1)
+    def _():
+        for e in range(len(final)):
+            for copy in onward(e):
+                copy.wait_send()
+
+    for k in range(half):
+        for o in range(len(leave)):
+
+            @pl.when(m == k)
+            def _(k=k, o=o):
+                stay(k, o).wait()
+
+            @pl.when(m != k)
+            def _(k=k, o=o):
+                done = deliver(k, o, k % 2, k // 2, k)
+                done.wait_send()
+                done.wait_recv()
+
+
+def waves(initial_state, source, absorption):
+    length = lax.axis_size("step")
+    windows = lax.axis_size("win")
+    nx, ny, nz = initial_state.shape
+    half = length // 2
+    reach = SWEEPS - 1
+    bs, bsy = nx // 2, ny // 2
+    ext = bs + reach
+    ey = bsy + TILE
+    units = length // 2
+    plan = spans(ext, bs, reach)
+    arrive, final, second, leave = (len(group) for group in plan)
+    f32 = jnp.float32
+    dma = pltpu.SemaphoreType.DMA
+    edge = pltpu.VMEM((bs, TILE, nz), f32)
+    return pl.pallas_call(
+        functools.partial(wave_kernel, length, windows, nx, ny, ext, ey, plan),
+        out_shape=jax.ShapeDtypeStruct((nx, ny, nz), f32),
+        in_specs=[pl.BlockSpec(memory_space=pltpu.HBM)] * 3,
+        out_specs=pl.BlockSpec(memory_space=pl.ANY),
+        scratch_shapes=[
+            pltpu.VMEM((nx, ny, nz), f32),
+            pltpu.VMEM((length, ext, ey, nz), f32),
+            pltpu.VMEM((ext, ey, nz), f32),
+            pltpu.VMEM((ext, ey, nz), f32),
+            pltpu.VMEM((3 * length // 4, ext, ey, nz), f32),
+            pltpu.VMEM((reach, units, ext + 2, ey + 2 * TILE, nz), f32),
+            pltpu.VMEM((units, bs, bsy, nz), f32),
+            pltpu.VMEM((ext, ey, nz), f32),
+            edge, edge, edge, edge, edge, edge,
+            pltpu.VMEM((half // 2, bs, bsy, nz), f32),
+            pltpu.VMEM((half // 2, bs, bsy, nz), f32),
+            pltpu.VMEM((half, bs, bsy, nz), f32),
+            dma((4,)),
+            dma((half, arrive)),
+            dma((length, arrive)),
+            dma((half, arrive)),
+            dma((final,)),
+            dma((final,)),
+            dma((2, final)),
+            dma((2, final)),
+            dma((7, final)),
+            dma((5, final)),
+            dma((half // 2, leave)),
+            dma((half // 2, leave)),
+            dma((half, leave)),
+            dma((half, leave)),
+            dma((leave,)),
+        ],
+        compiler_params=pltpu.CompilerParams(
+            collective_id=0, has_side_effects=True, vmem_limit_bytes=40 * 1024 * 1024
+        ),
+    )(source[0, 0], initial_state, absorption)[None, None]
+
+
 def fits(mesh, shape):
     length = mesh.shape["step"]
     if length % 8 or shape[2] != LANES or shape[1] != 4 * TILE:
@@ -555,9 +1112,15 @@
     return shape[0] % gx == 0 and shape[0] // gx >= SWEEPS - 1
 
 
+def pairs_up(mesh, shape):
+    return mesh.shape["step"] == 8 and shape[0] // 2 >= 2 * SWEEPS
+
+
 def solution(mesh):
     def body(initial_state, source, absorption):
-        plan = blocks if fits(mesh, initial_state.shape) else per_device
+        plan = per_device
+        if fits(mesh, initial_state.shape):
+            plan = waves if pairs_up(mesh, initial_state.shape) else blocks
         return plan(initial_state, source, absorption)
 
     return jax.shard_map(

time: 49.8 us -> 41.9 us (0.84)
  the two profiles are of different devices: /device:TPU:12 before, /device:TPU:0 now
where the time goes in v1:
time: 41.9 us; the launch traced here: 41.6 us
  Pallas kernels  37.7 us (90%)
  local copies, waits for them, and re-layouts  3.92 us (9%)
    pallas_call x1, Pallas kernels, waves(): pl.pallas_call(functools.partial(wave_kernel, length, windows, nx, ny, ex...  37.7 us
    unnamed x7, local copies, waits for them, and re-layouts  3.92 us

profile of v1, /device:TPU:0, one launch (start us, length us, event | category | flops | bytes accessed | tf_op | source)
XLA Modules:
  0.0 41.6 jit_solution(5258682503043424791)
XLA Ops:
  0.0 0.0 copy-start
  0.0 1.0 %copy-done = f32[1,1,32,32,128]{4,3,2,1,0:T(8,128)S(1)} copy-done((f32[1,1,32,32,128]{4,3,2,1,0:T(8,128)S(1)}, f32[1,1,32,32,128]{4,3,2,1,0:T(8,128)}, u32[]{:S(2)}) %copy-start) | copy-done | bytes 524312
  1.0 0.0 copy-start.1
  1.0 1.0 %copy-done.1 = f32[32,32,128]{2,1,0:T(8,128)S(1)} copy-done((f32[32,32,128]{2,1,0:T(8,128)S(1)}, f32[32,32,128]{2,1,0:T(8,128)}, u32[]{:S(2)}) %copy-start.1) | copy-done | bytes 524312
  2.1 0.0 copy-start.2
  2.1 1.0 %copy-done.2 = f32[32,32,128]{2,1,0:T(8,128)S(1)} copy-done((f32[32,32,128]{2,1,0:T(8,128)S(1)}, f32[32,32,128]{2,1,0:T(8,128)}, u32[]{:S(2)}) %copy-start.2) | copy-done | bytes 524312
  3.1 37.7 %shard_map.37 = f32[32,32,128]{2,1,0:T(8,128)S(1)} custom-call(f32[32,32,128]{2,1,0:T(8,128)S(1)} %bitcast.3, f32[32,32,128]{2,1,0:T(8,128)S(1)} %copy-done.1, f32[32,32,128]{2,1,0:T(8,128)S(1)} %copy-done.2), custom_call_target="tpu_custom_call" | custom-call | tf_op jit(solution)/shard_map/pallas_call | solution.py:1067
  40.8 0.8 %copy.5 = f32[1,1,32,32,128]{4,3,2,1,0:T(8,128)} copy(f32[1,1,32,32,128]{4,3,2,1,0:T(8,128)S(1)} %bitcast.2) | data formatting | bytes 1048576
Async XLA Ops:
  0.0 1.0 %copy-start = (f32[1,1,32,32,128]{4,3,2,1,0:T(8,128)S(1)}, f32[1,1,32,32,128]{4,3,2,1,0:T(8,128)}, u32[]{:S(2)}) copy-start(f32[1,1,32,32,128]{4,3,2,1,0:T(8,128)} %param.4) | copy-start | bytes 1572868
  1.0 1.0 %copy-start.1 = (f32[32,32,128]{2,1,0:T(8,128)S(1)}, f32[32,32,128]{2,1,0:T(8,128)}, u32[]{:S(2)}) copy-start(f32[32,32,128]{2,1,0:T(8,128)} %initial.1) | copy-start | bytes 1572868
  2.1 1.0 %copy-start.2 = (f32[32,32,128]{2,1,0:T(8,128)S(1)}, f32[32,32,128]{2,1,0:T(8,128)}, u32[]{:S(2)}) copy-start(f32[32,32,128]{2,1,0:T(8,128)} %absorb.1) | copy-start | bytes 1572868

commit v2 on v1

--- a/solution.py
+++ b/solution.py
@@ -547,28 +547,47 @@
     )(source[0, 0], initial_state, absorption)[None, None]
 
 
+ARRIVE = (8, 4, 3, 3, 3)
+SECOND = (5, 3, 3, 3, 3, 3)
+LEAST = 3
+
+
+def cuts(sizes, extent):
+    bounds = [0]
+    for size in sizes:
+        if bounds[-1] + size < extent:
+            bounds.append(bounds[-1] + size)
+    bounds.append(extent)
+    return list(zip(bounds[:-1], bounds[1:]))
+
+
 def spans(ext, bs, reach):
-    bounds = [0, *range(reach + 5, ext, 4), ext]
-    arrive = list(zip(bounds[:-1], bounds[1:]))
-    final = [(max(0, a - reach), b - reach) for a, b in arrive]
-    second = [(a, b, "own", e) for e, (a, b) in enumerate(final)]
-    for e in reversed(range(len(final))):
-        a, b = final[e]
+    arrive = cuts(ARRIVE, ext)
+    final = [(max(0, a - reach), b - reach) for a, b in arrive if b > reach]
+    sources = [(a, b, "own", e) for e, (a, b) in enumerate(final)]
+    for e, (a, b) in enumerate(final):
         if b > bs - reach:
-            a = max(a, bs - reach)
-            second.append((2 * bs - b, 2 * bs - a, "beyond", e))
-    leave = [(max(0, a - reach), b - reach) for a, b, _, _ in second if b > reach]
-    return arrive, final, second, leave
+            sources.append((2 * bs - b, 2 * bs - max(a, bs - reach), "beyond", e))
+    second, leave, after, sent = [], [], {}, 0
+    groups = cuts(SECOND, ext)
+    for g, (a, b) in enumerate(groups):
+        needs = [(kind, e) for lo, hi, kind, e in sources if a <= lo < b or (lo < a and g == 0)]
+        second.append((a, b, needs))
+        if b - reach - sent >= LEAST or g == len(groups) - 1:
+            after[g] = len(leave)
+            leave.append((sent, b - reach))
+            sent = b - reach
+    return arrive, final, second, leave, after
 
 
 def wave_kernel(
     length, windows, nx, ny, ext, ey, plan,
     source, initial, absorb, out,
-    srcv, raw, first, absv, coef, level, fin, corr,
-    emine, esend, egot, zgot, zother, csend, xsend, xgot, obuf,
-    lsem, asend, brecv, fsend, esem_s, esem_r, zsem_s, zsem_r, csem_s, csem_r, xsem_s, xsem_r, osem_s, osem_r, hsem,
+    srcv, raw, first, absv, coef, levels, fin, corr,
+    emine, esend, egot, zgot, csend, xsend, xgot, obuf,
+    lsem, asem, isem, fsem, dsem, esem_s, esem_r, zsem_s, zsem_r, csem_s, csem_r, bsem_r, xsem_s, xsem_r, osem, hsem,
 ):
-    arrive, final, second, leave = plan
+    arrive, final, second, leave, after = plan
     half = length // 2
     bs, bsy = nx // 2, ny // 2
     reach = SWEEPS - 1
@@ -614,7 +633,7 @@
     loads = [
         pltpu.make_async_copy(source, srcv, lsem.at[0]),
         pltpu.make_async_copy(region(absorb, bx, by, 0, ext), absv, lsem.at[1]),
-        pltpu.make_async_copy(region(source, bx, by, 0, ext), raw.at[me], lsem.at[2]),
+        pltpu.make_async_copy(region(source, bx, by, 0, ext), raw.at[core, m], lsem.at[2]),
         pltpu.make_async_copy(region(initial, bx, by, 0, ext), first, lsem.at[3]),
     ]
     for load in loads:
@@ -641,7 +660,6 @@
     @pl.when(w == 0)
     def _():
         zgot[...] = jnp.zeros_like(zgot)
-        zother[...] = jnp.zeros_like(zother)
 
     nearby = jnp.where(w > 0, 2, 0) + jnp.where(w < windows - 1, 2, 0)
     loads[0].wait()
@@ -653,11 +671,8 @@
             device_id=where, device_id_type=pl.DeviceIdType.MESH,
         )
 
-    outgoing = []
-
-    def launch(copy):
-        copy.start()
-        outgoing.append(copy)
+    def taken(block, sem):
+        return remote(block, block, sem, sem, step=partner)
 
     others = [(1, 1), (1, 0), (0, 1)]
 
@@ -665,35 +680,30 @@
         return (bx + ex) % 2, (by + e_y) % 2
 
     for c, (lo, hi) in enumerate(arrive):
-        for d, (ex, e_y) in enumerate(others):
-            tx, ty = beside(ex, e_y)
-            launch(
-                remote(
-                    region(srcv, tx, ty, lo, hi),
-                    raw.at[me, pl.ds(rows_of(lo, hi, tx), hi - lo)],
-                    asend.at[d, c], brecv.at[me, c], step=chip(tx, ty) * 2 + core,
-                )
-            )
-        here = pl.ds(rows_of(lo, hi), hi - lo)
-        launch(
+        for where in others:
+            tx, ty = beside(*where)
             remote(
-                region(srcv, bx, by, lo, hi), raw.at[me, here],
-                asend.at[len(others), c], brecv.at[me, c], step=partner,
-            )
-        )
+                region(srcv, tx, ty, lo, hi),
+                raw.at[core, m, pl.ds(rows_of(lo, hi, tx), hi - lo)],
+                asem, isem.at[c], step=chip(tx, ty) * 2 + core,
+            ).start()
 
     zero_row = jnp.zeros((ey, LANES), jnp.float32)
 
-    def rim(g, carry):
-        k, u = g // units, g % units
-        for r in (0, ext + 1):
-            level[k, u, r, pl.ds(TILE, ey)] = zero_row
-        for r in range(1, ext + 1):
-            level[k, u, r, pl.ds(0, TILE)] = zero_row[:TILE]
-            level[k, u, r, pl.ds(TILE + ey, TILE)] = zero_row[:TILE]
+    def rim(r, carry):
+        for refs in levels:
+            for ref in refs:
+                for q in range(2):
+                    ref[q, r, pl.ds(0, TILE)] = zero_row[:TILE]
+                    ref[q, r, pl.ds(TILE + ey, TILE)] = zero_row[:TILE]
         return carry
 
-    lax.fori_loop(0, reach * units, rim, 0)
+    for refs in levels:
+        for ref in refs:
+            for q in range(2):
+                for r in (0, ext + 1):
+                    ref[q, r, pl.ds(TILE, ey)] = zero_row
+    lax.fori_loop(1, ext + 1, rim, 0)
 
     def grouped(begin, count, work, most):
         groups = -(-count // most)
@@ -753,7 +763,8 @@
             folded = []
             for t in range(half):
                 early, late = gamma**t / coupling, gamma ** (t + half) / coupling
-                folded.append(early * raw[t, i] + pick(late, -late) * raw[t + half, i])
+                now, then = raw[t % 2, t // 2, i], raw[t % 2, (t + half) // 2, i]
+                folded.append(early * now + pick(late, -late) * then)
             folded[0] = folded[0] + first[i] * is_first
             for p in range(pairs):
                 weight = weights(p, i)
@@ -767,17 +778,17 @@
                 turn = [[tuple(round(v, 15) for v in pair) for pair in row] for row in turn]
                 s0 = combine(turn[0], folded)
                 s1 = combine(turn[1], folded)
-                level[0, 2 * p, i + 1, pl.ds(TILE, ey)] = weight[0] * s0 - weight[2] * s1
-                level[0, 2 * p + 1, i + 1, pl.ds(TILE, ey)] = weight[1] * s1 + weight[2] * s0
-
-    def stencil(k, u, start, rows, y0, depth):
+                levels[0][p][0, i + 1, pl.ds(TILE, ey)] = weight[0] * s0 - weight[2] * s1
+                levels[0][p][1, i + 1, pl.ds(TILE, ey)] = weight[1] * s1 + weight[2] * s0
+
+    def stencil(ref, q, start, rows, y0, depth):
         lane = lax.broadcasted_iota(jnp.int32, (depth, LANES), 1)
         at = pl.multiple_of(y0 + TILE, TILE)
-        line = [level[k, u, start + n, pl.ds(at, depth)] for n in range(rows + 2)]
+        line = [ref[q, start + n, pl.ds(at, depth)] for n in range(rows + 2)]
         sums = []
         for n in range(1, rows + 1):
             v = line[n]
-            around = level.at[k, u, start + n, pl.ds(y0, depth + 2 * TILE), :]
+            around = ref.at[q, start + n, pl.ds(y0, depth + 2 * TILE), :]
             total = jnp.where(lane == 0, 0.0, pltpu.roll(v, 1, 1))
             total = total + jnp.where(lane == LANES - 1, 0.0, pltpu.roll(v, LANES - 1, 1))
             across = around[pl.ds(TILE - 1, depth)] + around[pl.ds(TILE + 1, depth)]
@@ -789,21 +800,21 @@
         y0, depth = (oy, bsy) if last else (0, ey)
         at = pl.multiple_of(y0 + TILE, TILE)
         for p in range(pairs):
-            s0 = stencil(k - 1, 2 * p, start, rows, y0, depth)
-            s1 = stencil(k - 1, 2 * p + 1, start, rows, y0, depth)
+            s0 = stencil(levels[k - 1][p], 0, start, rows, y0, depth)
+            s1 = stencil(levels[k - 1][p], 1, start, rows, y0, depth)
             for n in range(rows):
                 i = start + n
                 weight = weights(p, i, y0, depth)
-                b0 = level[0, 2 * p, i + 1, pl.ds(at, depth)]
-                b1 = level[0, 2 * p + 1, i + 1, pl.ds(at, depth)]
+                b0 = levels[0][p][0, i + 1, pl.ds(at, depth)]
+                b1 = levels[0][p][1, i + 1, pl.ds(at, depth)]
                 v0 = b0 + (weight[0] * s0[n] - weight[2] * s1[n])
                 v1 = b1 + (weight[1] * s1[n] + weight[2] * s0[n])
                 if last:
-                    fin[2 * p, i - ox] = v0
-                    fin[2 * p + 1, i - ox] = v1
+                    fin[p][0, i - ox] = v0
+                    fin[p][1, i - ox] = v1
                 else:
-                    level[k, 2 * p, i + 1, pl.ds(TILE, ey)] = v0
-                    level[k, 2 * p + 1, i + 1, pl.ds(TILE, ey)] = v1
+                    levels[k][p][0, i + 1, pl.ds(TILE, ey)] = v0
+                    levels[k][p][1, i + 1, pl.ds(TILE, ey)] = v1
 
     def sweeps(a, b):
         for k in range(1, SWEEPS):
@@ -815,7 +826,7 @@
         total = None
         for u in range(units):
             factor = pick(back[0][t[0]][u], back[1][t[1]][u])
-            term = factor * fin[u, pl.ds(start, rows), pl.ds(y0, depth), :]
+            term = factor * fin[u // 2][u % 2, pl.ds(start, rows), pl.ds(y0, depth), :]
             total = term if total is None else total + term
         return total
 
@@ -824,20 +835,14 @@
 
     def swap(e):
         lo, hi = final[e]
-        return remote(strip(esend, lo, hi), strip(egot, lo, hi), esem_s.at[e], esem_r.at[e], step=partner)
+        return remote(strip(esend, lo, hi), strip(egot, lo, hi), esem_s, esem_r.at[e], step=partner)
 
     def onward(e):
         lo, hi = final[e]
-        after = (w + 1) % windows
+        after_w = (w + 1) % windows
         return [
-            remote(
-                strip(emine, lo, hi), strip(zgot, lo, hi),
-                zsem_s.at[0, e], zsem_r.at[0, e], win=after, step=me,
-            ),
-            remote(
-                strip(esend, lo, hi), strip(zother, lo, hi),
-                zsem_s.at[1, e], zsem_r.at[1, e], win=after, step=partner,
-            ),
+            remote(strip(emine, lo, hi), strip(zgot.at[0], lo, hi), zsem_s, zsem_r.at[e], win=after_w, step=me),
+            remote(strip(esend, lo, hi), strip(zgot.at[1], lo, hi), zsem_s, zsem_r.at[e], win=after_w, step=partner),
         ]
 
     def finish(e):
@@ -846,13 +851,14 @@
         start, rows = own_of(lo, hi), hi - lo
         esend[pl.ds(start, rows)] = part(last, start, rows, pl.multiple_of(TILE * (1 - core), TILE), TILE)
         emine[pl.ds(start, rows)] = part(last, start, rows, pl.multiple_of(TILE * core, TILE), TILE)
-        launch(swap(e))
 
         @pl.when(w < windows - 1)
         def _():
             for copy in onward(e):
                 copy.start()
 
+        swap(e).start()
+
     def landing(f_x, f_y, f_c, t_x, t_y, lo, hi):
         rows = pl.ds(f_x * bs + own_of(lo, hi, f_x) - xlo(t_x), hi - lo)
         depth = pl.ds(pl.multiple_of(f_y * bsy + TILE * f_c - ylo(t_y), TILE), TILE)
@@ -862,17 +868,15 @@
         lo, hi = final[e]
         return max(lo, bs - reach), hi
 
-    def spread(e, act):
+    def spread(e):
         lo, hi = final[e]
 
-        def one(slot, where, to_core, lo, hi, recv):
+        def one(where, to_core, lo, hi, send, recv):
             tx, ty = beside(*where)
-            act(
-                remote(
-                    strip(csend, lo, hi), landing(bx, by, core, tx, ty, lo, hi),
-                    csem_s.at[slot, e], csem_r.at[recv, e], step=chip(tx, ty) * 2 + to_core,
-                )
-            )
+            remote(
+                strip(csend, lo, hi), landing(bx, by, core, tx, ty, lo, hi),
+                send, recv, step=chip(tx, ty) * 2 + to_core,
+            ).start()
 
         lo2, hi2 = edge(e)
         if hi2 > lo2:
@@ -880,31 +884,33 @@
             @pl.when(near)
             def _():
                 for c in range(2):
-                    one(1 + c, (1, 1), c, lo2, hi2, 4)
+                    one((1, 1), c, lo2, hi2, csem_s.at[2], bsem_r.at[e])
 
             for c in range(2):
-                one(3 + c, (1, 0), c, lo2, hi2, 2 + core)
+                one((1, 0), c, lo2, hi2, csem_s.at[0], bsem_r.at[e])
 
         @pl.when(near)
         def _():
             for c in range(2):
-                one(5 + c, (0, 1), c, lo, hi, 1)
-
-        one(0, (0, 0), 1 - core, lo, hi, 0)
+                one((0, 1), c, lo, hi, csem_s.at[1], csem_r.at[e])
+
+        one((0, 0), 1 - core, lo, hi, csem_s.at[0], csem_r.at[e])
+
+    def spread_done():
+        taken(srcv.at[pl.ds(0, bs + 2 * reach), pl.ds(0, TILE), :], csem_s.at[0]).wait_send()
+
+        @pl.when(near)
+        def _():
+            taken(srcv.at[pl.ds(0, 2 * bs), pl.ds(0, TILE), :], csem_s.at[1]).wait_send()
+            taken(srcv.at[pl.ds(0, 2 * reach), pl.ds(0, TILE), :], csem_s.at[2]).wait_send()
 
     def gather(e, kind):
         lo, hi = final[e]
         if kind == "own":
-            sources = [(0, (0, 0), 1 - core), (1, (0, 1), by)]
+            taken(corr.at[pl.ds(0, hi - lo), pl.ds(0, 2 * TILE), :], csem_r.at[e]).wait_recv()
         else:
             lo, hi = edge(e)
-            sources = [(2, (1, 0), 0), (3, (1, 0), 1), (4, (1, 1), by)]
-        for slot, where, f_c in sources:
-            fx, fy = beside(*where)
-            remote(
-                strip(csend, lo, hi), landing(fx, fy, f_c, bx, by, lo, hi),
-                csem_s.at[0, e], csem_r.at[slot, e], step=partner,
-            ).wait_recv()
+            taken(corr.at[pl.ds(0, hi - lo)], bsem_r.at[e]).wait_recv()
 
     def change(e):
         lo, hi = final[e]
@@ -912,38 +918,13 @@
 
         @pl.when(w > 0)
         def _():
-            for copy in onward(e):
-                copy.wait_recv()
+            taken(zgot.at[:, pl.ds(0, hi - lo)], zsem_r.at[e]).wait_recv()
 
         mine = pl.ds(own_of(lo, hi), hi - lo)
-        value = (zgot[mine] + zother[mine]) - alpha_corner * (emine[mine] + egot[mine])
+        value = (zgot[0, mine] + zgot[1, mine]) - alpha_corner * (emine[mine] + egot[mine])
         csend[mine] = value
         corr[pl.ds(ox + own_of(lo, hi), hi - lo), pl.ds(pl.multiple_of(oy + TILE * core, TILE), TILE), :] = value
-        spread(e, lambda copy: copy.start())
-
-    def arrival(t, c):
-        lo, hi = arrive[c]
-        return raw.at[t, pl.ds(rows_of(lo, hi), hi - lo)]
-
-    for c, (a, b) in enumerate(arrive):
-        for d, (ex, e_y) in enumerate(others):
-            t = chip(*beside(ex, e_y)) * 2 + core
-            block = arrival(t, c)
-            copy = remote(block, block, fsend.at[d, c], brecv.at[t, c], step=partner)
-            copy.wait_recv()
-            launch(copy)
-        if c == 0:
-            loads[2].wait()
-            loads[3].wait()
-        for ex, e_y in [(0, 0), *others]:
-            t = chip(*beside(ex, e_y)) * 2 + (1 - core)
-            block = arrival(t, c)
-            remote(block, block, fsend.at[0, c], brecv.at[t, c], step=partner).wait_recv()
-        grouped(rows_of(a, b), b - a, spectrum, 3)
-        sweeps(a, b)
-        finish(c)
-        if c:
-            change(c - 1)
+        spread(e)
 
     def second_weight(p, weight):
         return weight[2] + (pick(1.0, 0.0) * weight[1] if p == 0 else 0.0)
@@ -955,22 +936,21 @@
             for p in range(pairs):
                 weight = weights(p, i)
                 spot = pl.ds(TILE, ey)
-                level[0, 2 * p, i + 1, spot] = level[0, 2 * p, i + 1, spot] + weight[0] * x
-                level[0, 2 * p + 1, i + 1, spot] = (
-                    level[0, 2 * p + 1, i + 1, spot] + second_weight(p, weight) * x
-                )
+                ref = levels[0][p]
+                ref[0, i + 1, spot] = ref[0, i + 1, spot] + weight[0] * x
+                ref[1, i + 1, spot] = ref[1, i + 1, spot] + second_weight(p, weight) * x
 
     def trade(i, o):
         lo, hi = leave[o]
         mine = pl.ds(own_of(lo, hi), hi - lo)
-        return remote(xsend.at[i, mine], xgot.at[i, mine], xsem_s.at[i, o], xsem_r.at[i, o], step=partner)
+        return remote(xsend.at[i, mine], xgot.at[i, mine], xsem_s, xsem_r.at[o], step=partner)
 
     def emit(o):
         lo, hi = leave[o]
         start, rows = own_of(lo, hi), hi - lo
         for i in range(kept):
             xsend[i, pl.ds(start, rows)] = part((2 * i + 1, 2 * i), start, rows, 0, bsy)
-            launch(trade(i, o))
+            trade(i, o).start()
         for i in range(kept):
             obuf[i, pl.ds(start, rows)] = part((2 * i, 2 * i + 1), start, rows, 0, bsy)
 
@@ -978,75 +958,89 @@
         rows = pl.ds(b_x * bs + own_of(lo, hi, b_x), hi - lo)
         return out.at[rows, pl.ds(pl.multiple_of(b_y * bsy, TILE), bsy), :]
 
-    def stay(k, o):
-        lo, hi = leave[o]
-        return pltpu.make_async_copy(strip(obuf.at[k], lo, hi), place(bx, by, lo, hi), hsem.at[o])
-
-    def deliver(k, o, b_x, b_y, slot):
-        lo, hi = leave[o]
-        return remote(
-            strip(obuf.at[k], lo, hi), place(b_x, b_y, lo, hi),
-            osem_s.at[k, o], osem_r.at[slot, o], step=2 * k + core,
-        )
-
-    ratio = gamma ** (-half)
-
     def settle(o):
         lo, hi = leave[o]
         mine = pl.ds(own_of(lo, hi), hi - lo)
+        ratio = gamma ** (-half)
+        taken(xgot.at[:, pl.ds(0, hi - lo)], xsem_r.at[o]).wait_recv()
         for i in range(kept):
-            trade(i, o).wait_recv()
             ours, theirs = obuf[i, mine], xgot[i, mine]
             obuf[i, mine] = ours + theirs
             obuf[i + kept, mine] = pick(ratio, -ratio) * (ours - theirs)
-            for k in (i, i + kept):
-
-                @pl.when(m == k)
-                def _(k=k):
-                    stay(k, o).start()
-
-                @pl.when(m != k)
-                def _(k=k):
-                    deliver(k, o, bx, by, m).start()
-
-    pending = len(final) - 1
-    o = -1
-    for g, (a, b, kind, e) in enumerate(second):
-        if kind == "own" and e == pending - 1:
-            change(pending)
-        gather(e, kind)
+        for where in others:
+            k = chip(*beside(*where))
+            remote(
+                strip(obuf.at[k], lo, hi), place(bx, by, lo, hi), osem.at[0], osem.at[1], step=2 * k + core
+            ).start()
+        pltpu.make_async_copy(strip(obuf.at[m], lo, hi), place(bx, by, lo, hi), hsem).start()
+
+    def receive(c):
+        lo, hi = arrive[c]
+        taken(raw.at[0, pl.ds(0, len(others)), pl.ds(0, hi - lo)], isem.at[c]).wait_recv()
+        block = raw.at[core, :, pl.ds(rows_of(lo, hi), hi - lo)]
+        remote(block, block, fsem, dsem.at[c], step=partner).start()
+
+    def advance(c):
+        a, b = arrive[c]
+        taken(raw.at[0, :, pl.ds(0, b - a)], dsem.at[c]).wait_recv()
+        grouped(rows_of(a, b), b - a, spectrum, 3)
+        sweeps(a, b)
+
+    waiting = []
+
+    def again(g):
+        a, b, needs = second[g]
+        for kind, e in needs:
+            gather(e, kind)
+        if waiting and ("own", ends - 2) in needs:
+            settle(waiting.pop())
         grouped(rows_of(a, b), b - a, correct, 5)
         sweeps(a, b)
-        if b > reach:
-            o += 1
-            emit(o)
-            if o:
-                settle(o - 1)
-    settle(o)
-
-    for copy in outgoing:
-        copy.wait_send()
-    for e in range(len(final)):
-        spread(e, lambda copy: copy.wait_send())
+        if g in after:
+            emit(after[g])
+            if waiting:
+                settle(waiting.pop())
+            waiting.append(after[g])
+
+    chunks, ends = len(arrive), len(final)
+
+    def step(c):
+        advance(c)
+        e = c - (chunks - ends)
+        if e >= 0:
+            finish(e)
+            if 1 <= e < ends - 1:
+                change(e - 1)
+
+    loads[2].wait()
+    loads[3].wait()
+    for c in range(chunks):
+        receive(c)
+        if c:
+            step(c - 1)
+    step(chunks - 1)
+    late = [ends - 2, ends - 1]
+    for g in range(len(second)):
+        while any(kind == "own" and e in late for kind, e in second[g][2]):
+            change(late.pop(0))
+        again(g)
+        if late:
+            change(late.pop(0))
+    settle(waiting.pop())
+
+    taken(raw.at[0, pl.ds(0, len(others))], asem).wait_send()
+    taken(raw.at[0], fsem).wait_send()
+    taken(esend, esem_s).wait_send()
+    spread_done()
 
     @pl.when(w < windows - 1)
     def _():
-        for e in range(len(final)):
-            for copy in onward(e):
-                copy.wait_send()
-
-    for k in range(half):
-        for o in range(len(leave)):
-
-            @pl.when(m == k)
-            def _(k=k, o=o):
-                stay(k, o).wait()
-
-            @pl.when(m != k)
-            def _(k=k, o=o):
-                done = deliver(k, o, k % 2, k // 2, k)
-                done.wait_send()
-                done.wait_recv()
+        taken(zgot, zsem_s).wait_send()
+
+    taken(xsend, xsem_s).wait_send()
+    taken(obuf.at[pl.ds(0, len(others))], osem.at[0]).wait_send()
+    taken(obuf.at[pl.ds(0, len(others))], osem.at[1]).wait_recv()
+    pltpu.make_async_copy(obuf.at[0], obuf.at[0], hsem).wait()
 
 
 def waves(initial_state, source, absorption):
@@ -1060,7 +1054,7 @@
     ey = bsy + TILE
     units = length // 2
     plan = spans(ext, bs, reach)
-    arrive, final, second, leave = (len(group) for group in plan)
+    arrive, final, _, leave, _ = (len(group) for group in plan)
     f32 = jnp.float32
     dma = pltpu.SemaphoreType.DMA
     edge = pltpu.VMEM((bs, TILE, nz), f32)
@@ -1071,37 +1065,40 @@
         out_specs=pl.BlockSpec(memory_space=pl.ANY),
         scratch_shapes=[
             pltpu.VMEM((nx, ny, nz), f32),
-            pltpu.VMEM((length, ext, ey, nz), f32),
+            pltpu.VMEM((2, half, ext, ey, nz), f32),
             pltpu.VMEM((ext, ey, nz), f32),
             pltpu.VMEM((ext, ey, nz), f32),
             pltpu.VMEM((3 * length // 4, ext, ey, nz), f32),
-            pltpu.VMEM((reach, units, ext + 2, ey + 2 * TILE, nz), f32),
-            pltpu.VMEM((units, bs, bsy, nz), f32),
+            [[pltpu.VMEM((2, ext + 2, ey + 2 * TILE, nz), f32)] * (units // 2)] * reach,
+            [pltpu.VMEM((2, bs, bsy, nz), f32)] * (units // 2),
             pltpu.VMEM((ext, ey, nz), f32),
-            edge, edge, edge, edge, edge, edge,
+            edge, edge, edge,
+            pltpu.VMEM((2, bs, TILE, nz), f32),
+            edge,
             pltpu.VMEM((half // 2, bs, bsy, nz), f32),
             pltpu.VMEM((half // 2, bs, bsy, nz), f32),
             pltpu.VMEM((half, bs, bsy, nz), f32),
             dma((4,)),
-            dma((half, arrive)),
-            dma((length, arrive)),
-            dma((half, arrive)),
+            dma,
+            dma((arrive,)),
+            dma,
+            dma((arrive,)),
+            dma,
+            dma((final,)),
+            dma,
+            dma((final,)),
+            dma((3,)),
             dma((final,)),
             dma((final,)),
-            dma((2, final)),
-            dma((2, final)),
-            dma((7, final)),
-            dma((5, final)),
-            dma((half // 2, leave)),
-            dma((half // 2, leave)),
-            dma((half, leave)),
-            dma((half, leave)),
+            dma,
             dma((leave,)),
+            dma((2,)),
+            dma,
         ],
         compiler_params=pltpu.CompilerParams(
             collective_id=0, has_side_effects=True, vmem_limit_bytes=40 * 1024 * 1024
         ),
-    )(source[0, 0], initial_state, absorption)[None, None]
+    )(*(pltpu.with_memory_space_constraint(x, pltpu.HBM) for x in (source[0, 0], initial_state, absorption)))[None, None]
 
 
 def fits(mesh, shape):

time: 41.9 us -> 34.2 us (0.82)
  Pallas kernels: 37.7 us -> 32.8 us
  local copies, waits for them, and re-layouts: 3.92 us -> 0.8 us
    pallas_call x1, Pallas kernels: 37.7 us -> 32.8 us  [waves(): pl.pallas_call(functools.partial(wave_kernel, length, windows, nx, ny, ex...]
    unnamed x7 -> x1, local copies, waits for them, and re-layouts: 3.92 us -> 0.8 us
where the time goes in v2:
time: 34.2 us; the launch traced here: 33.6 us
  Pallas kernels  32.8 us (96%)
  local copies, waits for them, and re-layouts  0.8 us (2%)
    pallas_call x1, Pallas kernels, waves(): pl.pallas_call(functools.partial(wave_kernel, length, windows, nx, ny, ex...  32.8 us
    unnamed x1, local copies, waits for them, and re-layouts  0.8 us

profile of v2, /device:TPU:0, one launch (start us, length us, event | category | flops | bytes accessed | tf_op | source)
XLA Modules:
  0.0 33.6 jit_solution(9158502389843071790)
XLA Ops:
  0.0 32.8 %shard_map.37 = f32[32,32,128]{2,1,0:T(8,128)S(1)} custom-call(f32[32,32,128]{2,1,0:T(8,128)} %bitcast.3, f32[32,32,128]{2,1,0:T(8,128)} %initial.1, f32[32,32,128]{2,1,0:T(8,128)} %absorb.1), custom_call_target="tpu_custom_call" | custom-call | tf_op jit(solution)/shard_map/pallas_call | solution.py:1061
  32.8 0.8 %copy.5 = f32[1,1,32,32,128]{4,3,2,1,0:T(8,128)} copy(f32[1,1,32,32,128]{4,3,2,1,0:T(8,128)S(1)} %bitcast.2) | data formatting | bytes 1048576

commit v3 on v2

--- a/solution.py
+++ b/solution.py
@@ -618,6 +618,12 @@
     def own_of(lo, hi, b=bx):
         return lo + b * (bs - lo - hi)
 
+    def held(i):
+        return i + bx * (ext - 1 - 2 * i)
+
+    def own(i):
+        return i + bx * (bs - 1 - 2 * i)
+
     def pick(a, b):
         if a == b:
             return jnp.float32(a)
@@ -726,7 +732,7 @@
         for n in range(rows):
             i = start + n
             for p in range(pairs):
-                here = absv[i]
+                here = absv[held(i)]
                 cosine = pick(math.cos(angles[0][p]), math.cos(angles[1][p]))
                 imag = pick(gamma * math.sin(angles[0][p]), gamma * math.sin(angles[1][p]))
                 real = 1.0 - gamma * cosine + here + 6.0 * coupling
@@ -763,9 +769,9 @@
             folded = []
             for t in range(half):
                 early, late = gamma**t / coupling, gamma ** (t + half) / coupling
-                now, then = raw[t % 2, t // 2, i], raw[t % 2, (t + half) // 2, i]
+                now, then = raw[t % 2, t // 2, held(i)], raw[t % 2, (t + half) // 2, held(i)]
                 folded.append(early * now + pick(late, -late) * then)
-            folded[0] = folded[0] + first[i] * is_first
+            folded[0] = folded[0] + first[held(i)] * is_first
             for p in range(pairs):
                 weight = weights(p, i)
                 turn = [
@@ -810,8 +816,8 @@
                 v0 = b0 + (weight[0] * s0[n] - weight[2] * s1[n])
                 v1 = b1 + (weight[1] * s1[n] + weight[2] * s0[n])
                 if last:
-                    fin[p][0, i - ox] = v0
-                    fin[p][1, i - ox] = v1
+                    fin[p][0, i] = v0
+                    fin[p][1, i] = v1
                 else:
                     levels[k][p][0, i + 1, pl.ds(TILE, ey)] = v0
                     levels[k][p][1, i + 1, pl.ds(TILE, ey)] = v1
@@ -820,15 +826,16 @@
         for k in range(1, SWEEPS):
             lo, hi = max(0, a - k), b - k
             if hi > lo:
-                grouped(rows_of(lo, hi), hi - lo, functools.partial(sweep_rows, k), 6)
-
-    def part(t, start, rows, y0, depth):
-        total = None
-        for u in range(units):
-            factor = pick(back[0][t[0]][u], back[1][t[1]][u])
-            term = factor * fin[u // 2][u % 2, pl.ds(start, rows), pl.ds(y0, depth), :]
-            total = term if total is None else total + term
-        return total
+                grouped(lo, hi - lo, functools.partial(sweep_rows, k), 6)
+
+    def part(ref, t, lo, hi, y0, depth):
+        factors = [pick(back[0][t[0]][u], back[1][t[1]][u]) for u in range(units)]
+        for i in range(lo, hi):
+            total = None
+            for u, factor in enumerate(factors):
+                term = factor * fin[u // 2][u % 2, i, pl.ds(y0, depth)]
+                total = term if total is None else total + term
+            ref[own(i)] = total
 
     def strip(ref, lo, hi):
         return ref.at[pl.ds(own_of(lo, hi), hi - lo)]
@@ -848,9 +855,8 @@
     def finish(e):
         lo, hi = final[e]
         last = (length - 1, length - 1)
-        start, rows = own_of(lo, hi), hi - lo
-        esend[pl.ds(start, rows)] = part(last, start, rows, pl.multiple_of(TILE * (1 - core), TILE), TILE)
-        emine[pl.ds(start, rows)] = part(last, start, rows, pl.multiple_of(TILE * core, TILE), TILE)
+        part(esend, last, lo, hi, pl.multiple_of(TILE * (1 - core), TILE), TILE)
+        part(emine, last, lo, hi, pl.multiple_of(TILE * core, TILE), TILE)
 
         @pl.when(w < windows - 1)
         def _():
@@ -932,7 +938,7 @@
     def correct(start, rows):
         for n in range(rows):
             i = start + n
-            x = corr[i] * (1.0 / coupling)
+            x = corr[held(i)] * (1.0 / coupling)
             for p in range(pairs):
                 weight = weights(p, i)
                 spot = pl.ds(TILE, ey)
@@ -947,12 +953,11 @@
 
     def emit(o):
         lo, hi = leave[o]
-        start, rows = own_of(lo, hi), hi - lo
         for i in range(kept):
-            xsend[i, pl.ds(start, rows)] = part((2 * i + 1, 2 * i), start, rows, 0, bsy)
+            part(xsend.at[i], (2 * i + 1, 2 * i), lo, hi, 0, bsy)
             trade(i, o).start()
         for i in range(kept):
-            obuf[i, pl.ds(start, rows)] = part((2 * i, 2 * i + 1), start, rows, 0, bsy)
+            part(obuf.at[i], (2 * i, 2 * i + 1), lo, hi, 0, bsy)
 
     def place(b_x, b_y, lo, hi):
         rows = pl.ds(b_x * bs + own_of(lo, hi, b_x), hi - lo)
@@ -983,7 +988,7 @@
     def advance(c):
         a, b = arrive[c]
         taken(raw.at[0, :, pl.ds(0, b - a)], dsem.at[c]).wait_recv()
-        grouped(rows_of(a, b), b - a, spectrum, 3)
+        grouped(a, b - a, spectrum, 3)
         sweeps(a, b)
 
     waiting = []
@@ -992,9 +997,7 @@
         a, b, needs = second[g]
         for kind, e in needs:
             gather(e, kind)
-        if waiting and ("own", ends - 2) in needs:
-            settle(waiting.pop())
-        grouped(rows_of(a, b), b - a, correct, 5)
+        grouped(a, b - a, correct, 5)
         sweeps(a, b)
         if g in after:
             emit(after[g])

time: 34.2 us -> 33.2 us (0.971)
  Pallas kernels: 32.8 us -> 31.9 us
    pallas_call x1, Pallas kernels: 32.8 us -> 31.9 us  [waves(): pl.pallas_call(functools.partial(wave_kernel, length, windows, nx, ny, ex...]
where the time goes in v3:
time: 33.2 us; the launch traced here: 32.7 us
  Pallas kernels  31.9 us (96%)
  local copies, waits for them, and re-layouts  0.8 us (2%)
    pallas_call x1, Pallas kernels, waves(): pl.pallas_call(functools.partial(wave_kernel, length, windows, nx, ny, ex...  31.9 us
    unnamed x1, local copies, waits for them, and re-layouts  0.8 us

profile of v3, /device:TPU:0, one launch (start us, length us, event | category | flops | bytes accessed | tf_op | source)
XLA Modules:
  0.0 32.7 jit_solution(14648563610767500043)
XLA Ops:
  0.0 31.9 %shard_map.37 = f32[32,32,128]{2,1,0:T(8,128)S(1)} custom-call(f32[32,32,128]{2,1,0:T(8,128)} %bitcast.3, f32[32,32,128]{2,1,0:T(8,128)} %initial.1, f32[32,32,128]{2,1,0:T(8,128)} %absorb.1), custom_call_target="tpu_custom_call" | custom-call | tf_op jit(solution)/shard_map/pallas_call | solution.py:1064
  31.9 0.8 %copy.5 = f32[1,1,32,32,128]{4,3,2,1,0:T(8,128)} copy(f32[1,1,32,32,128]{4,3,2,1,0:T(8,128)S(1)} %bitcast.2) | data formatting | bytes 1048576

commit v4 on v3

--- a/solution.py
+++ b/solution.py
@@ -549,7 +549,7 @@
 
 ARRIVE = (8, 4, 3, 3, 3)
 SECOND = (5, 3, 3, 3, 3, 3)
-LEAST = 3
+LEAST = 1
 
 
 def cuts(sizes, extent):
@@ -985,13 +985,18 @@
         block = raw.at[core, :, pl.ds(rows_of(lo, hi), hi - lo)]
         remote(block, block, fsem, dsem.at[c], step=partner).start()
 
+    waiting = []
+    chunks, ends = len(arrive), len(final)
+    late = list(range(ends))
+
     def advance(c):
         a, b = arrive[c]
         taken(raw.at[0, :, pl.ds(0, b - a)], dsem.at[c]).wait_recv()
+        e = c - (chunks - ends)
+        while late and late[0] <= min(e - 2, ends - 4):
+            change(late.pop(0))
         grouped(a, b - a, spectrum, 3)
         sweeps(a, b)
-
-    waiting = []
 
     def again(g):
         a, b, needs = second[g]
@@ -1005,15 +1010,11 @@
                 settle(waiting.pop())
             waiting.append(after[g])
 
-    chunks, ends = len(arrive), len(final)
-
     def step(c):
         advance(c)
         e = c - (chunks - ends)
         if e >= 0:
             finish(e)
-            if 1 <= e < ends - 1:
-                change(e - 1)
 
     loads[2].wait()
     loads[3].wait()
@@ -1022,7 +1023,7 @@
         if c:
             step(c - 1)
     step(chunks - 1)
-    late = [ends - 2, ends - 1]
+    change(late.pop(0))
     for g in range(len(second)):
         while any(kind == "own" and e in late for kind, e in second[g][2]):
             change(late.pop(0))

time: 33.2 us -> 33 us (level); the launches traced: 32.7 us -> 32.9 us
  no operation moved by 1% of the time
where the time goes in v4:
time: 33 us; the launch traced here: 32.9 us
  Pallas kernels  32.1 us (97%)
  local copies, waits for them, and re-layouts  0.8 us (2%)
    pallas_call x1, Pallas kernels, waves(): pl.pallas_call(functools.partial(wave_kernel, length, windows, nx, ny, ex...  32.1 us
    unnamed x1, local copies, waits for them, and re-layouts  0.8 us

profile of v4, /device:TPU:0, one launch (start us, length us, event | category | flops | bytes accessed | tf_op | source)
XLA Modules:
  0.0 32.9 jit_solution(15182227730399224424)
XLA Ops:
  0.0 32.1 %shard_map.37 = f32[32,32,128]{2,1,0:T(8,128)S(1)} custom-call(f32[32,32,128]{2,1,0:T(8,128)} %bitcast.3, f32[32,32,128]{2,1,0:T(8,128)} %initial.1, f32[32,32,128]{2,1,0:T(8,128)} %absorb.1), custom_call_target="tpu_custom_call" | custom-call | tf_op jit(solution)/shard_map/pallas_call | solution.py:1065
  32.1 0.8 %copy.5 = f32[1,1,32,32,128]{4,3,2,1,0:T(8,128)} copy(f32[1,1,32,32,128]{4,3,2,1,0:T(8,128)S(1)} %bitcast.2) | data formatting | bytes 1048576

commit v5 on v4

--- a/solution.py
+++ b/solution.py
@@ -547,7 +547,7 @@
     )(source[0, 0], initial_state, absorption)[None, None]
 
 
-ARRIVE = (8, 4, 3, 3, 3)
+ARRIVE = (7, 5, 3, 3, 3)
 SECOND = (5, 3, 3, 3, 3, 3)
 LEAST = 1
 
@@ -585,7 +585,7 @@
     source, initial, absorb, out,
     srcv, raw, first, absv, coef, levels, fin, corr,
     emine, esend, egot, zgot, csend, xsend, xgot, obuf,
-    lsem, asem, isem, fsem, dsem, esem_s, esem_r, zsem_s, zsem_r, csem_s, csem_r, bsem_r, xsem_s, xsem_r, osem, hsem,
+    lsem, asem, isem, fsem, dsem, esem_s, esem_r, zsem_s, zsem_r, csem_s, csem_r, bsem_r, xsem_s, osem, hsem,
 ):
     arrive, final, second, leave, after = plan
     half = length // 2
@@ -949,7 +949,7 @@
     def trade(i, o):
         lo, hi = leave[o]
         mine = pl.ds(own_of(lo, hi), hi - lo)
-        return remote(xsend.at[i, mine], xgot.at[i, mine], xsem_s, xsem_r.at[o], step=partner)
+        return remote(xsend.at[i, mine], xgot.at[i, mine], xsem_s, isem.at[o], step=partner)
 
     def emit(o):
         lo, hi = leave[o]
@@ -967,7 +967,7 @@
         lo, hi = leave[o]
         mine = pl.ds(own_of(lo, hi), hi - lo)
         ratio = gamma ** (-half)
-        taken(xgot.at[:, pl.ds(0, hi - lo)], xsem_r.at[o]).wait_recv()
+        taken(xgot.at[:, pl.ds(0, hi - lo)], isem.at[o]).wait_recv()
         for i in range(kept):
             ours, theirs = obuf[i, mine], xgot[i, mine]
             obuf[i, mine] = ours + theirs
@@ -1084,7 +1084,7 @@
             pltpu.VMEM((half, bs, bsy, nz), f32),
             dma((4,)),
             dma,
-            dma((arrive,)),
+            dma((max(arrive, leave),)),
             dma,
             dma((arrive,)),
             dma,
@@ -1095,7 +1095,6 @@
             dma((final,)),
             dma((final,)),
             dma,
-            dma((leave,)),
             dma((2,)),
             dma,
         ],

time: 33 us -> 32.9 us (level)
  no operation moved by 1% of the time
where the time goes in v5:
time: 32.9 us; the launch traced here: 32.8 us
  Pallas kernels  32 us (97%)
  local copies, waits for them, and re-layouts  0.8 us (2%)
    pallas_call x1, Pallas kernels, waves(): pl.pallas_call(functools.partial(wave_kernel, length, windows, nx, ny, ex...  32 us
    unnamed x1, local copies, waits for them, and re-layouts  0.8 us

profile of v5, /device:TPU:0, one launch (start us, length us, event | category | flops | bytes accessed | tf_op | source)
XLA Modules:
  0.0 32.8 jit_solution(1009257374474166855)
XLA Ops:
  0.0 32.0 %shard_map.37 = f32[32,32,128]{2,1,0:T(8,128)S(1)} custom-call(f32[32,32,128]{2,1,0:T(8,128)} %bitcast.3, f32[32,32,128]{2,1,0:T(8,128)} %initial.1, f32[32,32,128]{2,1,0:T(8,128)} %absorb.1), custom_call_target="tpu_custom_call" | custom-call | tf_op jit(solution)/shard_map/pallas_call | solution.py:1065
  32.0 0.8 %copy.5 = f32[1,1,32,32,128]{4,3,2,1,0:T(8,128)} copy(f32[1,1,32,32,128]{4,3,2,1,0:T(8,128)S(1)} %bitcast.2) | data formatting | bytes 1048576
